TPU v7x, 32 devices: a whole 2x2x4 slice. The times are simulated.
32 devices in a mesh: dp: 32 (over z, y, x, core).
Axes of the slice: x: 2, y: 2, z: 4, core: 2. Of those that a mesh axis runs over, the one named last changes fastest.
Arguments:
- x_embed: bfloat16 [2048, 768], P('dp')
- positions: int32 [2048], P('dp')
- k_cache: bfloat16 [2, 2048, 32, 12, 64], P(None, 'dp')
- v_cache: bfloat16 [2, 2048, 32, 12, 64], P(None, 'dp')
- ln1_gain: bfloat16 [2, 768], P(None, 'dp')
- ln1_bias: bfloat16 [2, 768], P(None, 'dp')
- ln2_gain: bfloat16 [2, 768], P(None, 'dp')
- ln2_bias: bfloat16 [2, 768], P(None, 'dp')
- w_qkv: bfloat16 [2, 768, 2304], P(None, 'dp')
- b_qkv: bfloat16 [2, 2304], P(None, 'dp')
- w_out: bfloat16 [2, 768, 768], P(None, 'dp')
- b_out: bfloat16 [2, 768], P(None, 'dp')
- w_in: bfloat16 [2, 768, 3072], P(None, 'dp')
- b_in: bfloat16 [2, 3072], P(None, 'dp')
- w_down: bfloat16 [2, 3072, 768], P(None, 'dp')
- b_down: bfloat16 [2, 768], P(None, 'dp')
- lnf_gain: bfloat16 [768], P('dp')
- lnf_bias: bfloat16 [768], P('dp')
Outputs:
- output 1: bfloat16 [2048, 768], P('dp')
- output 2: bfloat16 [2, 2048, 32, 12, 64], P(None, 'dp')
- output 3: bfloat16 [2, 2048, 32, 12, 64], P(None, 'dp')
All inputs are finite; a program needn't handle non-finite values.
Results may differ from a plain program's by a relative error of at most 0.0109312.
Values are sent between devices in bfloat16 or wider.
A program may use at most 1 GiB of HBM per device.

v0:
```python
import collections
import functools
import heapq
import itertools
import math
import jax
import jax.numpy as jnp
import numpy as np
from jax import lax
from jax.experimental import pallas as pl
from jax.experimental.pallas import tpu as pltpu
from jax.sharding import PartitionSpec as P

LN_EPS = 1e-5
ROPE_BASE = 10000.0
MESH = pl.DeviceIdType.MESH
F32, BF16 = jnp.float32, jnp.bfloat16
NZ = 4
Z, Y, X, C = 0, 1, 2, 3
DIMS = (4, 2, 2, 2)
VEC_ROWS = 24
ROWS, D, HEADS, HEAD, SLOTS, FF = 64, 768, 12, 64, 32, 3072
KEYS = HEADS * SLOTS
HID = FF // 2
SEQS = 8
BLOCKS = ROWS // SEQS
VMEM_LIMIT, VMEM_SMALL = 36 << 20, 1 << 20
FREQS = tuple(float(np.float32(1.0) / np.float32(ROPE_BASE) ** (np.float32(2 * i) / np.float32(16))) for i in range(8))
FIRST = 7
SENDS = 6


LINK, CORES = 46600.0, 300000.0
FIXED, FIXED_CORES, HOP = 1.6, 0.9, 0.75
WINDOW, SLACK = 6, -0.5
SEQUENCE = (
    ('vec', 0, 0), ('qkv', 0, 0), ('qkv', 0, 1), ('qkv', 0, 2), ('win', 0, 0), ('win', 0, 1), ('win', 0, 2), ('win', 0, 3),
    ('qkv', 1, 0), ('down', 0, 0), ('qkv', 1, 1), ('down', 0, 1), ('out', 0, 0), ('qkv', 1, 2),
    ('win', 1, 0), ('win', 1, 1), ('win', 1, 2), ('win', 1, 3), ('down', 1, 0), ('down', 1, 1), ('out', 1, 0))


def group_parts(family, l, i):
    zxy, zyx = (Z, X, Y), (Z, Y, X)
    if family == 'vec':
        return [(family, l, 0, 128, zxy)]
    if family == 'qkv' and l == 1:
        return [(family, l, 768 * i, 768, zxy)]
    if family == 'win':
        return [(family, l, 384 * i, 384, (Y, Z, X))]
    if family == 'down':
        return [(family, l, 384 * i, 384, (Z, X))]
    return [(family, l, 768 * i, 384, zxy), (family, l, 768 * i + 384, 384, zyx)]


def sends(spec, phase, chip):
    family, _, _, width, order = spec
    size = width * {'vec': VEC_ROWS * 4, 'down': 192}.get(family, 48)
    for d in order[:phase]:
        size *= DIMS[d]
    if phase == len(order):
        return [(chip, size, [chip])]
    out, d = [], order[phase]
    for k in range(1, DIMS[d]):
        to = tuple((v + k) % DIMS[d] if e == d else v for e, v in enumerate(chip))
        up = to[d] > chip[d]
        path = range(chip[d], to[d]) if up else range(chip[d], to[d], -1)
        out.append((to, size, [(d, up) + tuple(v if e == d else w for e, w in enumerate(chip)) for v in path]))
    return out


def arrivals(groups):
    chips = list(itertools.product(range(4), range(2), range(2)))
    free, heap, got, times, set_out = {}, [], collections.Counter(), collections.defaultdict(list), {}

    def send(now, chip, g, i, phase):
        for to, size, links in sends(groups[g][i], phase, chip):
            own = to == chip
            begin = max([now] + [free.get(k, 0.0) for k in links])
            end = begin + size / (CORES if own else LINK)
            for k in links:
                free[k] = end
            heapq.heappush(heap, (end + (FIXED_CORES if own else FIXED + HOP * (len(links) - 1)), len(times), next(ticket), to, g, i, phase))

    ticket = itertools.count()
    for chip in chips:
        for g in range(WINDOW):
            for i in range(len(groups[g])):
                send(0.0, chip, g, i, 0)
        set_out[chip] = WINDOW
    while heap:
        now, _, _, chip, g, i, phase = heapq.heappop(heap)
        got[chip, g, i, phase] += 1
        spec = groups[g][i]
        if got[chip, g, i, phase] < len(sends(spec, phase, chip)):
            continue
        times[g, i, phase].append(now)
        if phase < len(spec[4]):
            send(now, chip, g, i, phase + 1)
        if phase == 0:
            got[chip, g] += 1
            if got[chip, g] == len(groups[g]) and set_out[chip] < len(groups):
                later = set_out[chip]
                set_out[chip] += 1
                for j in range(len(groups[later])):
                    send(now, chip, later, j, 0)
    return sorted((sum(v) / len(v), k) for k, v in times.items())


def compute_tasks():
    out = {'vec': ([('vec', 0, 0)], [], 2.0)}
    for l in range(2):
        out[f's{l}'] = ([], ['o0'] if l else ['vec'], 0.3)
        for i in range(3):
            out[f'q{l}{i}'] = ([('qkv', l, i)], [f's{l}'], 0.6)
        out[f'h{l}'] = ([], [f'q{l}2'], 0.5)
        for i in range(4):
            out[f'w{l}{i}'] = ([('win', l, i)], [f'h{l}'], 0.5)
        for i in range(2):
            out[f'd{l}{i}'] = ([('down', l, i)], [f'w{l}{k}' for k in range(4)], 0.5)
        for i in range(BLOCKS):
            out[f'a{l}{i}'] = ([], [f'q{l}{k}' for k in range(3)], 1.2)
        out[f'o{l}'] = ([('out', l, 0)], [f'a{l}{k}' for k in range(BLOCKS)] + [f'd{l}0', f'd{l}1'], 0.6)
    return out


def make_plan():
    groups = [group_parts(*name) for name in SEQUENCE]
    specs = [spec for group in groups for spec in group]
    index = {(g, i): sum(len(h) for h in groups[:g]) + i for g, group in enumerate(groups) for i in range(len(group))}
    events, tasks = arrivals(groups), compute_tasks()
    steps = [(index[g, i], -1) for g in range(WINDOW) for i in range(len(groups[g]))]
    done, left, first_left, set_out, clock = set(), collections.Counter(), collections.Counter(), WINDOW, 0.0
    for g, group in enumerate(groups):
        left[g] = sum(len(spec[4]) + 1 for spec in group)
        first_left[g] = len(group)
    for n, (when, (g, i, phase)) in enumerate(events):
        clock = max(clock, when)
        steps.append((index[g, i], phase))
        left[g] -= 1
        if left[g] == 0:
            done.add(SEQUENCE[g])
        if phase == 0:
            first_left[g] -= 1
            if first_left[g] == 0 and set_out < len(groups):
                steps += [(index[set_out, j], -1) for j in range(len(groups[set_out]))]
                set_out += 1
        until = events[n + 1][0] + SLACK if n + 1 < len(events) else math.inf
        while clock < until:
            ready = [k for k, (needs, after, _) in tasks.items() if done.issuperset(needs) and done.issuperset(after)]
            if not ready:
                break
            steps.append(ready[0])
            done.add(ready[0])
            clock += tasks.pop(ready[0])[2]
    assert not tasks
    return specs, steps


class Part:
    def __init__(self, ref, lead, cols, order, where, sems, held=(Z, Y, X), first=None):
        self.ref, self.lead, self.cols, self.order, self.where = ref, lead, cols, order, where
        self.send_sems, self.recv_sems, self.index = sems
        self.held, self.first = held, first

    def block(self, full, where):
        sel = tuple(pl.ds(0, DIMS[d]) if d in full else where[d] for d in self.held)
        return self.ref.at[self.lead + sel + (where[C], slice(None), self.cols)]

    def device(self, d, value):
        w = list(self.where)
        w[d] = value
        return (((w[0] * 2 + w[1]) * 2 + w[2]) * 2 + w[3],)

    def copies(self, phase):
        d = self.order[phase] if phase < len(self.order) else C
        full = self.order[:phase]
        if self.order[0] == Y and phase > 0 and self.first is not None:
            full = (Y,) + tuple(self.order[1:phase])
        if d == Z:
            targets = [(k, (self.where[Z] + k + 1) % NZ) for k in range(NZ - 1)]
        else:
            targets = [({X: 3, Y: 4, C: 5}[d], 1 - self.where[d])]
        blk = self.block(full, self.where)
        src = self.first if (phase == 0 and self.first is not None) else blk
        return [pltpu.make_async_remote_copy(
            src_ref=src, dst_ref=blk, send_sem=self.send_sems.at[self.index, k], recv_sem=self.recv_sems.at[self.index, k],
            device_id=self.device(d, to), device_id_type=MESH) for k, to in targets]

    @property
    def phases(self):
        return len(self.order) + 1

    def start(self, phase):
        for cp in self.copies(phase):
            cp.start()

    def finish(self, phase):
        for cp in self.copies(phase):
            cp.wait_recv()

    def drain(self):
        for phase in range(self.phases):
            for cp in self.copies(phase):
                cp.wait_send()


def iota(shape, axis):
    return lax.broadcasted_iota(jnp.int32, shape, axis)


def floor_div(values, width):
    return jnp.floor((values + 0.5) * (1.0 / width))


def dot(a, b):
    return jnp.dot(a, b, preferred_element_type=F32)


def layer_norm(x_f32, gain, bias):
    row_mean = jnp.mean(x_f32, axis=-1, keepdims=True)
    centered = x_f32 - row_mean
    row_var = jnp.mean(centered * centered, axis=-1, keepdims=True)
    return (centered * lax.rsqrt(row_var + LN_EPS) * gain + bias).astype(BF16)


def one_hot_cols(width, cols_f32):
    index = cols_f32 - floor_div(cols_f32, width) * width
    return (iota(index.shape, 0).astype(F32) == index).astype(BF16)


def kernel(specs, steps, pos_ref, x_ref, g1_ref, c1_ref, g2_ref, c2_ref, bo_ref, bd_ref, gf_ref, cf_ref, bq_ref, bi_ref, qkv_ref, out_ref, win_ref, down_ref, k_hbm, v_hbm,
           y_ref, kbuf, vbuf,
           vec_g, qkv_g, out_g, win_g, down_g, x1_scr, xn_scr, ps_scr, pr_scr, h1_scr, h2_scr, act_scr, acc_scr,
           rope_ref, pos_scr, vrow_scr, bq_scr, bi_scr, q_scr, kn_scr, vn_scr, ctx_scr, s_scr,
           own_sem, send_sems, recv_sems, xs_sem, xr_sem, ps_sem, pr_sem, in_sem):
    me = lax.axis_index('dp')
    where = (me // 8, (me // 4) % 2, (me // 2) % 2, me % 2)
    z, y, x, c = where

    def device(z, y, x, c):
        return (((z * 2 + y) * 2 + x) * 2 + c,)

    y_peer = device(z, 1 - y, x, c)

    def cache_in(i):
        l, rows = i // BLOCKS, pl.ds(i % BLOCKS * SEQS, SEQS)
        return [pltpu.make_async_copy(k_hbm.at[l, rows], kbuf.at[l, rows], in_sem.at[0, i]),
                pltpu.make_async_copy(v_hbm.at[l, rows], vbuf.at[l, rows], in_sem.at[1, i])]

    def my_cols(zb, yy):
        return pl.ds(pl.multiple_of(768 * zb + 384 * yy, 128), 384)

    own = [(qkv_ref.at[0], qkv_g.at[0, z, y, x, c])]
    own += [(win_ref.at[0, :, my_cols(zb, y)], win_g.at[0, z, y, x, c, :, pl.ds(384 * zb, 384)]) for zb in range(4)]
    own += [(down_ref.at[0], down_g.at[0, z, x, c]), (out_ref.at[0], out_g.at[0, z, y, x, c]), (qkv_ref.at[1], qkv_g.at[1, z, y, x, c])]
    own += [(win_ref.at[1, :, my_cols(zb, y)], win_g.at[1, z, y, x, c, :, pl.ds(384 * zb, 384)]) for zb in range(4)]
    own += [(down_ref.at[1], down_g.at[1, z, x, c]), (out_ref.at[1], out_g.at[1, z, y, x, c])]
    own = [pltpu.make_async_copy(src, dst, own_sem.at[i]) for i, (src, dst) in enumerate(own)]
    for cp in own:
        cp.start()

    barrier = pltpu.get_barrier_semaphore()
    peers = [device((z + k) % NZ, y, x, c) for k in range(1, NZ)] + [device(z, y, 1 - x, c), y_peer, device(z, y, x, 1 - c)]
    for who in peers:
        pl.semaphore_signal(barrier, inc=1, device_id=who, device_id_type=MESH)

    own_vec = vec_g.at[0, z, y, x, c]
    own_vec[...] = jnp.zeros((VEC_ROWS, 128), F32)
    at_row = 0
    for ref in (g1_ref, c1_ref, g2_ref, c2_ref, bo_ref, bd_ref, gf_ref, cf_ref, bq_ref, bi_ref):
        count, width = ref.shape
        own_vec[pl.ds(at_row, count), pl.ds(0, width)] = ref[...].astype(F32)
        at_row += count

    pl.semaphore_wait(barrier, len(peers))
    for cp in own:
        cp.wait()
    for i in range(2 * BLOCKS):
        for cp in cache_in(i):
            cp.start()

    refs = {'vec': vec_g, 'qkv': qkv_g, 'win': win_g, 'down': down_g, 'out': out_g}
    parts = []
    for i, (family, l, col, width, order) in enumerate(specs):
        kw = {}
        if family == 'down':
            kw['held'] = (Z, X)
        if family == 'win':
            kw['first'] = win_ref.at[l, :, my_cols(col // 384, 1 - y)]
        parts.append(Part(refs[family], (l,), pl.ds(col, width), order, where, (send_sems, recv_sems, i), **kw))

    lane = iota((1, 128), 1)

    def send_x(l):
        src = x_ref if l == 0 else x1_scr
        return pltpu.make_async_remote_copy(src_ref=src, dst_ref=xn_scr.at[l], send_sem=xs_sem.at[l], recv_sem=xr_sem.at[l],
                                            device_id=y_peer, device_id_type=MESH)

    def send_part(l):
        return pltpu.make_async_remote_copy(src_ref=ps_scr.at[l], dst_ref=pr_scr.at[l], send_sem=ps_sem.at[l], recv_sem=pr_sem.at[l],
                                            device_id=y_peer, device_id_type=MESH)

    def task_rope():
        for b in range(ROWS):
            pos_scr[pl.ds(b, 1), :] = jnp.full((1, 128), pos_ref[b], jnp.int32).astype(F32)
        d = lane % HEAD
        freq = jnp.zeros((1, 128), F32)
        for i, f in enumerate(FREQS):
            freq = jnp.where(d % 8 == i, f, freq)
        angle = pos_scr[...] * freq
        cos, sin = jnp.cos(angle), jnp.sin(angle)
        for t, turned in enumerate((lane >= 0, lane >= 64, lane < 64)):
            rope_ref[3 * t] = jnp.where(turned & (d < 16), cos, 1.0)
            rope_ref[3 * t + 1] = jnp.where(turned & (d < 8), -sin, 0.0)
            rope_ref[3 * t + 2] = jnp.where(turned & (d >= 8) & (d < 16), sin, 0.0)

    def task_vec():
        vec2 = vec_g[...].reshape(32 * VEC_ROWS, 128).astype(BF16)
        n = iota((1, D), 1).astype(F32)
        spread = dot(vec2, one_hot_cols(24, jnp.broadcast_to(n, (128, D))))
        r = iota((32 * VEC_ROWS, 1), 0).astype(F32)
        mine = floor_div(n, 24) == floor_div(r, VEC_ROWS)
        spread = jnp.where(mine, spread, 0.0).astype(BF16)
        rr = iota((1, 32 * VEC_ROWS), 1).astype(F32)
        kind = rr - floor_div(rr, VEC_ROWS) * VEC_ROWS
        pick = (iota((VEC_ROWS, 32 * VEC_ROWS), 0).astype(F32) == kind).astype(BF16)
        vrow_scr[...] = dot(pick, spread)
        dev = iota((32, 1), 0).astype(F32)

        def long_row(kind, width, cols):
            g = vec_g[0, :, :, :, :, kind].reshape(32, 128).astype(BF16)
            n = cols.astype(F32)
            full = dot(g, one_hot_cols(width, jnp.broadcast_to(n, (128, n.shape[1]))))
            return jnp.sum(jnp.where(floor_div(n, width) == dev, full, 0.0), axis=0, keepdims=True)

        for l in range(2):
            bq_scr[l] = long_row(14 + l, 72, iota((1, 3 * D), 1))
            for zb in range(4):
                bi_scr[l, :, pl.ds(384 * zb, 384)] = long_row(16 + l, 96, iota((1, 384), 1) + (768 * zb + 384 * y))

    def vrow(kind):
        return vrow_scr[pl.ds(kind, 1), :]

    def x_of(l):
        return (x_ref if l == 0 else x1_scr)[...]

    def task_start(l):
        send_x(l).start()
        h1_scr[...] = layer_norm(x_of(l).astype(F32), vrow(l), vrow(2 + l))

    def task_qkv(l, i):
        w = qkv_g[l, :, :, :, :, :, pl.ds(768 * i, 768)].reshape(D, 768)
        got = (dot(h1_scr[...], w) + bq_scr[l, :, pl.ds(768 * i, 768)]).astype(BF16).astype(F32)
        for m in range(2):
            tiles = []
            for t in range(3):
                v = got[:, 384 * m + 128 * t: 384 * m + 128 * t + 128]
                r = v * rope_ref[3 * t] + pltpu.roll(v, 120, 1) * rope_ref[3 * t + 1] + pltpu.roll(v, 8, 1) * rope_ref[3 * t + 2]
                tiles.append(r.astype(BF16).astype(F32))
            h = 4 * i + 2 * m
            t0, t1, t2 = tiles
            q_scr[pl.ds(h, ROWS, stride=16), :] = t0
            kn_scr[pl.ds(h, ROWS, stride=16), :] = pltpu.roll(t0, 64, 1)
            vn_scr[pl.ds(h, ROWS, stride=16), :] = t1
            q_scr[pl.ds(h + 1, ROWS, stride=16), :] = pltpu.roll(t1, 64, 1)
            kn_scr[pl.ds(h + 1, ROWS, stride=16), :] = t2
            vn_scr[pl.ds(h + 1, ROWS, stride=16), :] = pltpu.roll(t2, 64, 1)

    def task_att(l, blk):
        for cp in cache_in(l * BLOCKS + blk):
            cp.wait()
        key = iota((1, KEYS), 1)
        head_row = jnp.minimum(iota((16, 1), 0), HEADS - 1) * SLOTS
        slot_of = key - head_row
        own_head = (slot_of >= 0) & (slot_of < SLOTS)
        slots = iota((SLOTS, HEAD), 0)

        def scores(j):
            b = blk * SEQS + j
            pos = pos_ref[b]
            rows = pl.ds(b * 16, 16)
            put = jnp.where(slots == pos, 1.0, 0.0).astype(BF16) > 0.5

            def placed(buf, new_scr):
                new = new_scr[rows, :][:HEADS, :HEAD].astype(BF16)
                both = jnp.where(put[None], new[:, None, :], buf[l, blk * SEQS + j])
                buf[l, blk * SEQS + j] = both
                return both.reshape(KEYS, HEAD)

            keys = placed(kbuf, kn_scr)
            placed(vbuf, vn_scr)
            q = q_scr[rows, :][:, :HEAD].astype(BF16)
            s = lax.dot_general(q, keys, (((1,), (1,)), ((), ())), preferred_element_type=F32) * (HEAD ** -0.5)
            s_scr[pl.ds(j * 16, 16), :] = jnp.where(own_head & (slot_of <= pos), s, -jnp.inf)

        def weighted(j):
            p = s_scr[pl.ds(j * 16, 16), :].astype(BF16)
            got = dot(p, vbuf[l, blk * SEQS + j].reshape(KEYS, HEAD))
            ctx_scr[pl.ds((blk * SEQS + j) * 16, 16), pl.ds(0, HEAD)] = got

        for j in range(SEQS):
            scores(j)
        s = s_scr[...]
        e = jnp.exp(s - jnp.max(s, axis=-1, keepdims=True))
        s_scr[...] = e / jnp.sum(e, axis=-1, keepdims=True)
        for j in range(SEQS):
            weighted(j)

    def task_h2(l):
        send_x(l).wait_recv()
        for half, v in enumerate((x_of(l), xn_scr[l])):
            h2_scr[pl.ds(ROWS * half, ROWS), :] = layer_norm(v.astype(F32), vrow(4 + l), vrow(6 + l))

    def task_win(l, zb):
        cols = pl.ds(384 * zb, 384)
        w = win_g[l, :, :, :, :, :, cols].reshape(D, 384)
        u = dot(h2_scr[...], w) + bi_scr[l, :, cols]
        act_scr[:, cols] = (0.5 * u * (1.0 + lax.erf(u * 0.7071067811865476))).astype(BF16)

    def task_down(l, i):
        cols = pl.ds(384 * i, 384)
        got = dot(act_scr[...], down_g[l, :, :, :, :, cols].reshape(HID, 384))
        acc_scr[:, cols] = got[:ROWS]
        ps_scr[l, :, cols] = got[ROWS:]
        if i == 1:
            send_part(l).start()

    def task_out(l):
        tiles = []
        for m in range(HEADS // 2):
            a = ctx_scr[pl.ds(2 * m, ROWS, stride=16), :]
            b = pltpu.roll(ctx_scr[pl.ds(2 * m + 1, ROWS, stride=16), :], 64, 1)
            tiles.append(jnp.where(lane < 64, a, b).astype(BF16))
        a = dot(jnp.concatenate(tiles, axis=1), out_g[l].reshape(D, D)) + vrow(8 + l)
        send_part(l).wait_recv()
        m = acc_scr[...] + pr_scr[l] + vrow(10 + l)
        new = (x_of(l).astype(F32) + a + m).astype(BF16)
        if l == 0:
            x1_scr[...] = new
        else:
            y_ref[...] = layer_norm(new.astype(F32), vrow(12), vrow(13))

    tasks = {'vec': task_vec}
    for l in range(2):
        tasks[f's{l}'] = functools.partial(task_start, l)
        tasks[f'h{l}'] = functools.partial(task_h2, l)
        tasks[f'o{l}'] = functools.partial(task_out, l)
        for name, fn, count in (('q', task_qkv, 3), ('w', task_win, 4), ('d', task_down, 2), ('a', task_att, BLOCKS)):
            for i in range(count):
                tasks[f'{name}{l}{i}'] = functools.partial(fn, l, i)

    for n, step in enumerate(steps):
        if isinstance(step, str):
            tasks.pop(step)()
            continue
        p, phase = parts[step[0]], step[1]
        if phase >= 0:
            p.finish(phase)
        if phase + 1 < p.phases:
            p.start(phase + 1)
        if n == FIRST:
            task_rope()
    assert not tasks

    for p in parts:
        p.drain()
    for l in range(2):
        send_x(l).wait_send()
        send_part(l).wait_send()


def write_kernel(y_ref, k_ref, v_ref, y_hbm, k_hbm, v_hbm, sem):
    copies = [pltpu.make_async_copy(y_ref, y_hbm, sem.at[0])]
    for ref, hbm in ((k_ref, k_hbm), (v_ref, v_hbm)):
        for l in range(2):
            for i in range(4):
                rows = pl.ds(16 * i, 16)
                copies.append(pltpu.make_async_copy(ref.at[l, rows], hbm.at[l, rows], sem.at[len(copies)]))
    for cp in copies:
        cp.start()
    for cp in copies:
        cp.wait()


def fused(pos, x, vecs, w_qkv, w_out, w_in, w_down, k_cache, v_cache):
    specs, steps = make_plan()
    parts = len(specs)
    vmem = pl.BlockSpec(memory_space=pltpu.VMEM)
    hbm = pl.BlockSpec(memory_space=pl.ANY)
    lead = (4, 2, 2, 2)
    dma = pltpu.SemaphoreType.DMA
    outs = (x, k_cache, v_cache)
    y, k_new, v_new = pl.pallas_call(
        functools.partial(kernel, specs, steps),
        out_shape=tuple(pltpu.VMEM(a.shape, a.dtype) for a in outs),
        in_specs=[pl.BlockSpec(memory_space=pltpu.SMEM), vmem] + [vmem] * len(vecs) + [hbm] * 6,
        out_specs=[vmem] * 3,
        scratch_shapes=[
            pltpu.VMEM((1,) + lead + (VEC_ROWS, 128), F32),
            pltpu.VMEM((2,) + lead + (24, 3 * D), BF16),
            pltpu.VMEM((2,) + lead + (24, D), BF16),
            pltpu.VMEM((2,) + lead + (24, HID), BF16),
            pltpu.VMEM((2, 4, 2, 2, 96, D), BF16),
            pltpu.VMEM((ROWS, D), BF16),
            pltpu.VMEM((2, ROWS, D), BF16),
            pltpu.VMEM((2, ROWS, D), F32),
            pltpu.VMEM((2, ROWS, D), F32),
            pltpu.VMEM((ROWS, D), BF16),
            pltpu.VMEM((2 * ROWS, D), BF16),
            pltpu.VMEM((2 * ROWS, HID), BF16),
            pltpu.VMEM((ROWS, D), F32),
            pltpu.VMEM((9, ROWS, 128), F32),
            pltpu.VMEM((ROWS, 128), F32),
            pltpu.VMEM((VEC_ROWS, D), F32),
            pltpu.VMEM((2, 1, 3 * D), F32),
            pltpu.VMEM((2, 1, HID), F32),
            pltpu.VMEM((16 * ROWS, 128), F32),
            pltpu.VMEM((16 * ROWS, 128), F32),
            pltpu.VMEM((16 * ROWS, 128), F32),
            pltpu.VMEM((16 * ROWS, 128), F32),
            pltpu.VMEM((16 * SEQS, KEYS), F32),
            dma((16,)), dma((parts, SENDS)), dma((parts, SENDS)), dma((2,)), dma((2,)), dma((2,)), dma((2,)), dma((2, 2 * BLOCKS)),
        ],
        compiler_params=pltpu.CompilerParams(collective_id=0, has_side_effects=True, vmem_limit_bytes=VMEM_LIMIT),
    )(pos, x, *vecs, w_qkv, w_out, w_in, w_down, k_cache, v_cache)
    return pl.pallas_call(
        write_kernel,
        out_shape=tuple(jax.ShapeDtypeStruct(a.shape, a.dtype) for a in outs),
        in_specs=[vmem] * 3,
        out_specs=[hbm] * 3,
        scratch_shapes=[dma((17,))],
        compiler_params=pltpu.CompilerParams(vmem_limit_bytes=VMEM_SMALL),
    )(y, k_new, v_new)


def solution(mesh):
    row_spec = P('dp', None)
    vec_spec = P(None, 'dp')
    mat_spec = P(None, 'dp', None)
    cache_spec = P(None, 'dp', None, None, None)
    in_specs = (row_spec, P('dp'), cache_spec, cache_spec, vec_spec, vec_spec, vec_spec, vec_spec, mat_spec, vec_spec, mat_spec, vec_spec, mat_spec, vec_spec, mat_spec, vec_spec, P('dp'), P('dp'))
    out_specs = (row_spec, cache_spec, cache_spec)

    def device_step(x_embed, positions, k_cache, v_cache, ln1_gain, ln1_bias, ln2_gain, ln2_bias, w_qkv, b_qkv, w_out, b_out, w_in, b_in, w_down, b_down, lnf_gain, lnf_bias):
        vecs = (ln1_gain, ln1_bias, ln2_gain, ln2_bias, b_out, b_down, lnf_gain[None], lnf_bias[None], b_qkv, b_in)
        by_head = lambda a: jnp.swapaxes(a, 2, 3)
        out, k_new, v_new = fused(positions, x_embed, vecs, w_qkv, w_out, w_in, w_down, by_head(k_cache), by_head(v_cache))
        return out, by_head(k_new), by_head(v_new)

    return jax.shard_map(device_step, mesh=mesh, in_specs=in_specs, out_specs=out_specs, check_vma=False)
```

profile of v0, /device:TPU:0, one launch (start us, length us, event | category | flops | bytes accessed | tf_op | source)
XLA Modules:
  0.0 136.4 jit_solution(14457240090378053157)
XLA Ops:
  0.6 127.0 %shard_map.193 = (bf16[64,768]{1,0:T(8,128)(2,1)S(1)}, bf16[2,64,12,32,64]{4,3,2,1,0:T(8,128)(2,1)S(1)}, bf16[2,64,12,32,64]{4,3,2,1,0:T(8,128)(2,1)S(1)}) custom-call(s32[64]{0:T(128)} %pos_ref.1, bf16[64,768]{1,0:T(8,128)(2,1)} %x_ref.1, bf16[2,24]{1,0:T(2,128)(2,1)} %g1_ref.1, bf16[2,24]{1,0:T(2,128)(2,1)} %c1_ref.1, bf16[2,24]{1,0:T(2,128)(2,1)} %g2_ref.1, ...), custom_call_target="tpu_custom_call" | custom-call | tf_op jit(solution)/shard_map/pallas_call | solution.py:493
  127.7 8.6 %shard_map.194 = (bf16[64,768]{1,0:T(8,128)(2,1)}, bf16[2,64,12,32,64]{4,3,2,1,0:T(8,128)(2,1)}, bf16[2,64,12,32,64]{4,3,2,1,0:T(8,128)(2,1)}) custom-call(bf16[64,768]{1,0:T(8,128)(2,1)S(1)} %get-tuple-element.9.y_ref, bf16[2,64,12,32,64]{4,3,2,1,0:T(8,128)(2,1)S(1)} %get-tuple-element.10.k_ref, bf16[2,64,12,32,64]{4,3,2,1,0:T(8,128)(2,1)S(1)} %get-tuple-element.11.v_ref), custom_call_target="tpu_custom_call" | custom-call | tf_op jit(solution)/shard_map/pallas_call | solution.py:526
where the time goes:
time: 137 us; the launch traced here: 136 us
  Pallas kernels  136 us (99%)
    pallas_call x1, Pallas kernels, fused(): pl.pallas_call(functools.partial(kernel, specs, steps), out_shape=tuple((...  127 us
    pallas_call x1, Pallas kernels, fused(): pl.pallas_call(write_kernel, out_shape=tuple((jax.ShapeDtypeStruct(a.shap...  8.55 us

commit v1 on v0

--- a/solution.py
+++ b/solution.py
@@ -17,6 +17,8 @@
 F32, BF16 = jnp.float32, jnp.bfloat16
 NZ = 4
 Z, Y, X, C = 0, 1, 2, 3
+Z1, Z2, Z3 = 4, 5, 6
+ALONG_Z = (Z1, Z2, Z3)
 DIMS = (4, 2, 2, 2)
 VEC_ROWS = 24
 ROWS, D, HEADS, HEAD, SLOTS, FF = 64, 768, 12, 64, 32, 3072
@@ -27,83 +29,100 @@
 VMEM_LIMIT, VMEM_SMALL = 36 << 20, 1 << 20
 FREQS = tuple(float(np.float32(1.0) / np.float32(ROPE_BASE) ** (np.float32(2 * i) / np.float32(16))) for i in range(8))
 FIRST = 7
-SENDS = 6
+SENDS = 9
 
 
 LINK, CORES = 46600.0, 300000.0
-FIXED, FIXED_CORES, HOP = 1.6, 0.9, 0.75
-WINDOW, SLACK = 6, -0.5
-SEQUENCE = (
-    ('vec', 0, 0), ('qkv', 0, 0), ('qkv', 0, 1), ('qkv', 0, 2), ('win', 0, 0), ('win', 0, 1), ('win', 0, 2), ('win', 0, 3),
-    ('qkv', 1, 0), ('down', 0, 0), ('qkv', 1, 1), ('down', 0, 1), ('out', 0, 0), ('qkv', 1, 2),
-    ('win', 1, 0), ('win', 1, 1), ('win', 1, 2), ('win', 1, 3), ('down', 1, 0), ('down', 1, 1), ('out', 1, 0))
+FIXED, FIXED_CORES = 1.6, 0.9
+WINDOW, SLACK = 3, -0.5
+ZXY, ZYX, XYZ, YXZ = ALONG_Z + (X, Y), ALONG_Z + (Y, X), (X, Y) + ALONG_Z, (Y, X) + ALONG_Z
+YZX, ZX, XZ = (Y,) + ALONG_Z + (X,), ALONG_Z + (X,), (X,) + ALONG_Z
+SHARES = {
+    'vec': [((1, ZXY),)],
+    'qkv': [((3, ZXY), (3, ZYX)), ((6, ZXY),)],
+    'out': [((6, ZXY),), ((6, ZXY),)],
+    'win': [((3, YZX),)] * 2,
+    'down': [((2, ZX), (1, XZ))] * 2,
+}
+GROUPS = tuple((f, l, i) for f, layers, n in (('vec', 1, 1), ('qkv', 2, 3), ('win', 2, 4), ('down', 2, 2), ('out', 2, 1)) for l in range(layers) for i in range(n))
+SEQUENCE = tuple(GROUPS[ord(k) - ord('a')] for k in 'cbaegqldhijfktnospmur')
 
 
 def group_parts(family, l, i):
-    zxy, zyx = (Z, X, Y), (Z, Y, X)
-    if family == 'vec':
-        return [(family, l, 0, 128, zxy)]
-    if family == 'qkv' and l == 1:
-        return [(family, l, 768 * i, 768, zxy)]
-    if family == 'win':
-        return [(family, l, 384 * i, 384, (Y, Z, X))]
-    if family == 'down':
-        return [(family, l, 384 * i, 384, (Z, X))]
-    return [(family, l, 768 * i, 384, zxy), (family, l, 768 * i + 384, 384, zyx)]
+    out, at = [], {'qkv': D, 'win': HID // 4, 'down': D // 2}.get(family, 0) * i
+    for units, order in SHARES[family][l]:
+        out.append((family, l, at, units * 128, order))
+        at += units * 128
+    return out
+
+
+def gathered(order, phase):
+    return {Z if d == Z3 else d for d in order[:phase]} - {Z1, Z2}
 
 
 def sends(spec, phase, chip):
     family, _, _, width, order = spec
-    size = width * {'vec': VEC_ROWS * 4, 'down': 192}.get(family, 48)
-    for d in order[:phase]:
+    size, z = width * {'vec': VEC_ROWS * 4, 'down': 192}.get(family, 48), chip[Z]
+    for d in gathered(order, phase):
         size *= DIMS[d]
     if phase == len(order):
-        return [(chip, size, [chip])]
-    out, d = [], order[phase]
-    for k in range(1, DIMS[d]):
-        to = tuple((v + k) % DIMS[d] if e == d else v for e, v in enumerate(chip))
-        up = to[d] > chip[d]
-        path = range(chip[d], to[d]) if up else range(chip[d], to[d], -1)
-        out.append((to, size, [(d, up) + tuple(v if e == d else w for e, w in enumerate(chip)) for v in path]))
-    return out
+        return [(chip, size, chip)]
+    axis = order[phase]
+    if axis in ALONG_Z:
+        hop, out = axis - Z1, []
+        if hop <= z < NZ - 1:
+            out.append(((z + 1,) + chip[1:], size, (Z, True) + chip))
+        if 0 < z < NZ - hop:
+            out.append(((z - 1,) + chip[1:], size, (Z, False) + chip))
+        return out
+    to = tuple(1 - v if e == axis else v for e, v in enumerate(chip))
+    return [(to, size, (axis,) + chip)]
+
+
+def comes(order, phase, chip):
+    if phase == len(order) or order[phase] not in ALONG_Z:
+        return 1
+    hop = order[phase] - Z1
+    return (chip[Z] > hop) + (chip[Z] + hop + 1 < NZ)
 
 
 def arrivals(groups):
     chips = list(itertools.product(range(4), range(2), range(2)))
-    free, heap, got, times, set_out = {}, [], collections.Counter(), collections.defaultdict(list), {}
+    free, heap, got, at, times = {}, [], collections.Counter(), collections.Counter(), collections.defaultdict(list)
+    set_out, ticket = {chip: WINDOW for chip in chips}, itertools.count()
 
     def send(now, chip, g, i, phase):
-        for to, size, links in sends(groups[g][i], phase, chip):
+        for to, size, link in sends(groups[g][i], phase, chip):
             own = to == chip
-            begin = max([now] + [free.get(k, 0.0) for k in links])
-            end = begin + size / (CORES if own else LINK)
-            for k in links:
-                free[k] = end
-            heapq.heappush(heap, (end + (FIXED_CORES if own else FIXED + HOP * (len(links) - 1)), len(times), next(ticket), to, g, i, phase))
-
-    ticket = itertools.count()
+            free[link] = max(now, free.get(link, 0.0)) + size / (CORES if own else LINK)
+            heapq.heappush(heap, (free[link] + (FIXED_CORES if own else FIXED), next(ticket), to, g, i, phase))
+
     for chip in chips:
         for g in range(WINDOW):
             for i in range(len(groups[g])):
                 send(0.0, chip, g, i, 0)
-        set_out[chip] = WINDOW
     while heap:
-        now, _, _, chip, g, i, phase = heapq.heappop(heap)
+        now, _, chip, g, i, phase = heapq.heappop(heap)
         got[chip, g, i, phase] += 1
-        spec = groups[g][i]
-        if got[chip, g, i, phase] < len(sends(spec, phase, chip)):
-            continue
-        times[g, i, phase].append(now)
-        if phase < len(spec[4]):
-            send(now, chip, g, i, phase + 1)
-        if phase == 0:
-            got[chip, g] += 1
-            if got[chip, g] == len(groups[g]) and set_out[chip] < len(groups):
-                later = set_out[chip]
-                set_out[chip] += 1
-                for j in range(len(groups[later])):
-                    send(now, chip, later, j, 0)
-    return sorted((sum(v) / len(v), k) for k, v in times.items())
+        order = groups[g][i][4]
+        while at[chip, g, i] <= len(order) and got[chip, g, i, at[chip, g, i]] == comes(order, at[chip, g, i], chip):
+            over = at[chip, g, i]
+            times[g, i, over].append(now)
+            at[chip, g, i] += 1
+            if over < len(order):
+                send(now, chip, g, i, over + 1)
+            if over == 0:
+                got[chip, g] += 1
+                if got[chip, g] == len(groups[g]) and set_out[chip] < len(groups):
+                    later = set_out[chip]
+                    set_out[chip] += 1
+                    for j in range(len(groups[later])):
+                        send(now, chip, later, j, 0)
+    mean = {k: sum(v) / len(v) for k, v in times.items()}
+    for g, i, phase in sorted(mean):
+        if phase:
+            mean[g, i, phase] = max(mean[g, i, phase], mean[g, i, phase - 1])
+    return sorted((v, k) for k, v in mean.items())
 
 
 def compute_tasks():
@@ -162,46 +181,50 @@
         self.send_sems, self.recv_sems, self.index = sems
         self.held, self.first = held, first
 
-    def block(self, full, where):
-        sel = tuple(pl.ds(0, DIMS[d]) if d in full else where[d] for d in self.held)
-        return self.ref.at[self.lead + sel + (where[C], slice(None), self.cols)]
-
-    def device(self, d, value):
+    def copy(self, phase, axis, to, slot, z):
+        full = gathered(self.order, phase)
+        if self.first is not None and phase > 0:
+            full.add(Y)
+        at = (z,) + self.where[1:]
+        sel = tuple(pl.ds(0, DIMS[d]) if d in full else at[d] for d in self.held)
+        blk = self.ref.at[self.lead + sel + (self.where[C], slice(None), self.cols)]
         w = list(self.where)
-        w[d] = value
-        return (((w[0] * 2 + w[1]) * 2 + w[2]) * 2 + w[3],)
-
-    def copies(self, phase):
-        d = self.order[phase] if phase < len(self.order) else C
-        full = self.order[:phase]
-        if self.order[0] == Y and phase > 0 and self.first is not None:
-            full = (Y,) + tuple(self.order[1:phase])
-        if d == Z:
-            targets = [(k, (self.where[Z] + k + 1) % NZ) for k in range(NZ - 1)]
-        else:
-            targets = [({X: 3, Y: 4, C: 5}[d], 1 - self.where[d])]
-        blk = self.block(full, self.where)
-        src = self.first if (phase == 0 and self.first is not None) else blk
-        return [pltpu.make_async_remote_copy(
-            src_ref=src, dst_ref=blk, send_sem=self.send_sems.at[self.index, k], recv_sem=self.recv_sems.at[self.index, k],
-            device_id=self.device(d, to), device_id_type=MESH) for k, to in targets]
+        w[axis] = to
+        return pltpu.make_async_remote_copy(
+            src_ref=self.first if phase == 0 and self.first is not None else blk, dst_ref=blk,
+            send_sem=self.send_sems.at[self.index, slot], recv_sem=self.recv_sems.at[self.index, slot],
+            device_id=((((w[0] * 2 + w[1]) * 2 + w[2]) * 2 + w[3]),), device_id_type=MESH)
+
+    def copies(self, phase, mine):
+        axis, z = self.order[phase] if phase < len(self.order) else C, self.where[Z]
+        if axis not in ALONG_Z:
+            return [(None, self.copy(phase, axis, 1 - self.where[axis], {X: 6, Y: 7, C: 8}[axis], z))]
+        hop = axis - Z1
+        if mine:
+            return [((z >= hop) & (z < NZ - 1), self.copy(phase, Z, z + 1, hop, z - hop)),
+                    ((z + hop < NZ) & (z > 0), self.copy(phase, Z, z - 1, 3 + hop, z + hop))]
+        return [(z > hop, self.copy(phase, Z, z, hop, z - hop - 1)), (z + hop + 1 < NZ, self.copy(phase, Z, z, 3 + hop, z + hop + 1))]
 
     @property
     def phases(self):
         return len(self.order) + 1
 
+    def each(self, phase, mine, act):
+        for condition, cp in self.copies(phase, mine):
+            if condition is None:
+                act(cp)
+            else:
+                pl.when(condition)(functools.partial(act, cp))
+
     def start(self, phase):
-        for cp in self.copies(phase):
-            cp.start()
+        self.each(phase, True, lambda cp: cp.start())
 
     def finish(self, phase):
-        for cp in self.copies(phase):
-            cp.wait_recv()
+        self.each(phase, False, lambda cp: cp.wait_recv())
 
     def drain(self):
         for phase in range(self.phases):
-            for cp in self.copies(phase):
-                cp.wait_send()
+            self.each(phase, True, lambda cp: cp.wait_send())
 
 
 def iota(shape, axis):
@@ -260,10 +283,12 @@
         cp.start()
 
     barrier = pltpu.get_barrier_semaphore()
-    peers = [device((z + k) % NZ, y, x, c) for k in range(1, NZ)] + [device(z, y, 1 - x, c), y_peer, device(z, y, x, 1 - c)]
-    for who in peers:
+    for who in (device(z, y, 1 - x, c), y_peer, device(z, y, x, 1 - c)):
         pl.semaphore_signal(barrier, inc=1, device_id=who, device_id_type=MESH)
-
+    for there, step in ((z > 0, -1), (z < NZ - 1, 1)):
+        @pl.when(there)
+        def _(step=step):
+            pl.semaphore_signal(barrier, inc=1, device_id=device(z + step, y, x, c), device_id_type=MESH)
     own_vec = vec_g.at[0, z, y, x, c]
     own_vec[...] = jnp.zeros((VEC_ROWS, 128), F32)
     at_row = 0
@@ -272,7 +297,7 @@
         own_vec[pl.ds(at_row, count), pl.ds(0, width)] = ref[...].astype(F32)
         at_row += count
 
-    pl.semaphore_wait(barrier, len(peers))
+    pl.semaphore_wait(barrier, 3 + (z + 3) // 4 + (6 - z) // 4)
     for cp in own:
         cp.wait()
     for i in range(2 * BLOCKS):
@@ -286,7 +311,7 @@
         if family == 'down':
             kw['held'] = (Z, X)
         if family == 'win':
-            kw['first'] = win_ref.at[l, :, my_cols(col // 384, 1 - y)]
+            kw['first'] = win_ref.at[l, :, pl.ds(pl.multiple_of(768 * (col // 384) + 384 * (1 - y) + col % 384, 128), width)]
         parts.append(Part(refs[family], (l,), pl.ds(col, width), order, where, (send_sems, recv_sems, i), **kw))
 
     lane = iota((1, 128), 1)
@@ -296,9 +321,10 @@
         return pltpu.make_async_remote_copy(src_ref=src, dst_ref=xn_scr.at[l], send_sem=xs_sem.at[l], recv_sem=xr_sem.at[l],
                                             device_id=y_peer, device_id_type=MESH)
 
-    def send_part(l):
-        return pltpu.make_async_remote_copy(src_ref=ps_scr.at[l], dst_ref=pr_scr.at[l], send_sem=ps_sem.at[l], recv_sem=pr_sem.at[l],
-                                            device_id=y_peer, device_id_type=MESH)
+    def send_part(l, i):
+        cols = pl.ds(384 * i, 384)
+        return pltpu.make_async_remote_copy(src_ref=ps_scr.at[l, :, cols], dst_ref=pr_scr.at[l, :, cols], send_sem=ps_sem.at[l, i],
+                                            recv_sem=pr_sem.at[l, i], device_id=y_peer, device_id_type=MESH)
 
     def task_rope():
         for b in range(ROWS):
@@ -422,8 +448,7 @@
         got = dot(act_scr[...], down_g[l, :, :, :, :, cols].reshape(HID, 384))
         acc_scr[:, cols] = got[:ROWS]
         ps_scr[l, :, cols] = got[ROWS:]
-        if i == 1:
-            send_part(l).start()
+        send_part(l, i).start()
 
     def task_out(l):
         tiles = []
@@ -432,7 +457,8 @@
             b = pltpu.roll(ctx_scr[pl.ds(2 * m + 1, ROWS, stride=16), :], 64, 1)
             tiles.append(jnp.where(lane < 64, a, b).astype(BF16))
         a = dot(jnp.concatenate(tiles, axis=1), out_g[l].reshape(D, D)) + vrow(8 + l)
-        send_part(l).wait_recv()
+        for i in range(2):
+            send_part(l, i).wait_recv()
         m = acc_scr[...] + pr_scr[l] + vrow(10 + l)
         new = (x_of(l).astype(F32) + a + m).astype(BF16)
         if l == 0:
@@ -466,7 +492,8 @@
         p.drain()
     for l in range(2):
         send_x(l).wait_send()
-        send_part(l).wait_send()
+        for i in range(2):
+            send_part(l, i).wait_send()
 
 
 def write_kernel(y_ref, k_ref, v_ref, y_hbm, k_hbm, v_hbm, sem):
@@ -519,7 +546,7 @@
             pltpu.VMEM((16 * ROWS, 128), F32),
             pltpu.VMEM((16 * ROWS, 128), F32),
             pltpu.VMEM((16 * SEQS, KEYS), F32),
-            dma((16,)), dma((parts, SENDS)), dma((parts, SENDS)), dma((2,)), dma((2,)), dma((2,)), dma((2,)), dma((2, 2 * BLOCKS)),
+            dma((16,)), dma((parts, SENDS)), dma((parts, SENDS)), dma((2,)), dma((2,)), dma((2, 2)), dma((2, 2)), dma((2, 2 * BLOCKS)),
         ],
         compiler_params=pltpu.CompilerParams(collective_id=0, has_side_effects=True, vmem_limit_bytes=VMEM_LIMIT),
     )(pos, x, *vecs, w_qkv, w_out, w_in, w_down, k_cache, v_cache)

time: 137 us -> 115 us (0.84)
  Pallas kernels: 136 us -> 114 us
    pallas_call x1, Pallas kernels: 127 us -> 105 us  [fused(): pl.pallas_call(functools.partial(kernel, specs, steps), out_shape=tuple((...]
where the time goes in v1:
time: 115 us
  Pallas kernels  114 us (99%)
    pallas_call x1, Pallas kernels, fused(): pl.pallas_call(functools.partial(kernel, specs, steps), out_shape=tuple((...  105 us
    pallas_call x1, Pallas kernels, fused(): pl.pallas_call(write_kernel, out_shape=tuple((jax.ShapeDtypeStruct(a.shap...  8.55 us

profile of v1, /device:TPU:0, one launch (start us, length us, event | category | flops | bytes accessed | tf_op | source)
XLA Modules:
  0.0 114.7 jit_solution(1691134734149935875)
XLA Ops:
  0.6 105.4 %shard_map.193 = (bf16[64,768]{1,0:T(8,128)(2,1)S(1)}, bf16[2,64,12,32,64]{4,3,2,1,0:T(8,128)(2,1)S(1)}, bf16[2,64,12,32,64]{4,3,2,1,0:T(8,128)(2,1)S(1)}) custom-call(s32[64]{0:T(128)} %pos_ref.1, bf16[64,768]{1,0:T(8,128)(2,1)} %x_ref.1, bf16[2,24]{1,0:T(2,128)(2,1)} %g1_ref.1, bf16[2,24]{1,0:T(2,128)(2,1)} %c1_ref.1, bf16[2,24]{1,0:T(2,128)(2,1)} %g2_ref.1, ...), custom_call_target="tpu_custom_call" | custom-call | tf_op jit(solution)/shard_map/pallas_call | solution.py:520
  106.0 8.6 %shard_map.194 = (bf16[64,768]{1,0:T(8,128)(2,1)}, bf16[2,64,12,32,64]{4,3,2,1,0:T(8,128)(2,1)}, bf16[2,64,12,32,64]{4,3,2,1,0:T(8,128)(2,1)}) custom-call(bf16[64,768]{1,0:T(8,128)(2,1)S(1)} %get-tuple-element.9.y_ref, bf16[2,64,12,32,64]{4,3,2,1,0:T(8,128)(2,1)S(1)} %get-tuple-element.10.k_ref, bf16[2,64,12,32,64]{4,3,2,1,0:T(8,128)(2,1)S(1)} %get-tuple-element.11.v_ref), custom_call_target="tpu_custom_call" | custom-call | tf_op jit(solution)/shard_map/pallas_call | solution.py:553

commit v2 on v1

--- a/solution.py
+++ b/solution.py
@@ -28,24 +28,24 @@
 BLOCKS = ROWS // SEQS
 VMEM_LIMIT, VMEM_SMALL = 36 << 20, 1 << 20
 FREQS = tuple(float(np.float32(1.0) / np.float32(ROPE_BASE) ** (np.float32(2 * i) / np.float32(16))) for i in range(8))
-FIRST = 7
+FIRST = 4
 SENDS = 9
 
 
 LINK, CORES = 46600.0, 300000.0
 FIXED, FIXED_CORES = 1.6, 0.9
-WINDOW, SLACK = 3, -0.5
+WINDOW, SLACK = 3, -1
 ZXY, ZYX, XYZ, YXZ = ALONG_Z + (X, Y), ALONG_Z + (Y, X), (X, Y) + ALONG_Z, (Y, X) + ALONG_Z
 YZX, ZX, XZ = (Y,) + ALONG_Z + (X,), ALONG_Z + (X,), (X,) + ALONG_Z
 SHARES = {
     'vec': [((1, ZXY),)],
-    'qkv': [((3, ZXY), (3, ZYX)), ((6, ZXY),)],
+    'qkv': [((6, ZXY),), ((6, ZXY),)],
     'out': [((6, ZXY),), ((6, ZXY),)],
     'win': [((3, YZX),)] * 2,
     'down': [((2, ZX), (1, XZ))] * 2,
 }
 GROUPS = tuple((f, l, i) for f, layers, n in (('vec', 1, 1), ('qkv', 2, 3), ('win', 2, 4), ('down', 2, 2), ('out', 2, 1)) for l in range(layers) for i in range(n))
-SEQUENCE = tuple(GROUPS[ord(k) - ord('a')] for k in 'cbaegqldhijfktnospmur')
+SEQUENCE = tuple(GROUPS[ord(k) - ord('a')] for k in 'tcbjakdligfhsequopmnr')
 
 
 def group_parts(family, l, i):
@@ -126,18 +126,18 @@
 
 
 def compute_tasks():
-    out = {'vec': ([('vec', 0, 0)], [], 2.0)}
+    out = {'vec': ([('vec', 0, 0)], [], 1.1)}
     for l in range(2):
-        out[f's{l}'] = ([], ['o0'] if l else ['vec'], 0.3)
+        out[f's{l}'] = ([], ['o0'] if l else ['vec'], 0.25)
         for i in range(3):
-            out[f'q{l}{i}'] = ([('qkv', l, i)], [f's{l}'], 0.6)
-        out[f'h{l}'] = ([], [f'q{l}2'], 0.5)
+            out[f'q{l}{i}'] = ([('qkv', l, i)], [f's{l}'], 0.4)
+        out[f'h{l}'] = ([], [f's{l}'], 0.4)
         for i in range(4):
-            out[f'w{l}{i}'] = ([('win', l, i)], [f'h{l}'], 0.5)
+            out[f'w{l}{i}'] = ([('win', l, i)], [f'h{l}'], 0.3)
         for i in range(2):
-            out[f'd{l}{i}'] = ([('down', l, i)], [f'w{l}{k}' for k in range(4)], 0.5)
+            out[f'd{l}{i}'] = ([('down', l, i)], [f'w{l}{k}' for k in range(4)], 0.4)
         for i in range(BLOCKS):
-            out[f'a{l}{i}'] = ([], [f'q{l}{k}' for k in range(3)], 1.2)
+            out[f'a{l}{i}'] = ([], [f'q{l}{k}' for k in range(3)], 0.7)
         out[f'o{l}'] = ([('out', l, 0)], [f'a{l}{k}' for k in range(BLOCKS)] + [f'd{l}0', f'd{l}1'], 0.6)
     return out
 
@@ -300,10 +300,6 @@
     pl.semaphore_wait(barrier, 3 + (z + 3) // 4 + (6 - z) // 4)
     for cp in own:
         cp.wait()
-    for i in range(2 * BLOCKS):
-        for cp in cache_in(i):
-            cp.start()
-
     refs = {'vec': vec_g, 'qkv': qkv_g, 'win': win_g, 'down': down_g, 'out': out_g}
     parts = []
     for i, (family, l, col, width, order) in enumerate(specs):
@@ -485,6 +481,9 @@
         if phase + 1 < p.phases:
             p.start(phase + 1)
         if n == FIRST:
+            for i in range(2 * BLOCKS):
+                for cp in cache_in(i):
+                    cp.start()
             task_rope()
     assert not tasks
 

time: 115 us -> 111 us (0.965)
  Pallas kernels: 114 us -> 110 us
    pallas_call x1, Pallas kernels: 105 us -> 102 us  [fused(): pl.pallas_call(functools.partial(kernel, specs, steps), out_shape=tuple((...]
where the time goes in v2:
time: 111 us
  Pallas kernels  110 us (99%)
    pallas_call x1, Pallas kernels, fused(): pl.pallas_call(functools.partial(kernel, specs, steps), out_shape=tuple((...  102 us
    pallas_call x1, Pallas kernels, fused(): pl.pallas_call(write_kernel, out_shape=tuple((jax.ShapeDtypeStruct(a.shap...  8.55 us

profile of v2, /device:TPU:0, one launch (start us, length us, event | category | flops | bytes accessed | tf_op | source)
XLA Modules:
  0.0 111.2 jit_solution(16106329210829848662)
XLA Ops:
  0.6 101.8 %shard_map.193 = (bf16[64,768]{1,0:T(8,128)(2,1)S(1)}, bf16[2,64,12,32,64]{4,3,2,1,0:T(8,128)(2,1)S(1)}, bf16[2,64,12,32,64]{4,3,2,1,0:T(8,128)(2,1)S(1)}) custom-call(s32[64]{0:T(128)} %pos_ref.1, bf16[64,768]{1,0:T(8,128)(2,1)} %x_ref.1, bf16[2,24]{1,0:T(2,128)(2,1)} %g1_ref.1, bf16[2,24]{1,0:T(2,128)(2,1)} %c1_ref.1, bf16[2,24]{1,0:T(2,128)(2,1)} %g2_ref.1, ...), custom_call_target="tpu_custom_call" | custom-call | tf_op jit(solution)/shard_map/pallas_call | solution.py:519
  102.5 8.6 %shard_map.194 = (bf16[64,768]{1,0:T(8,128)(2,1)}, bf16[2,64,12,32,64]{4,3,2,1,0:T(8,128)(2,1)}, bf16[2,64,12,32,64]{4,3,2,1,0:T(8,128)(2,1)}) custom-call(bf16[64,768]{1,0:T(8,128)(2,1)S(1)} %get-tuple-element.9.y_ref, bf16[2,64,12,32,64]{4,3,2,1,0:T(8,128)(2,1)S(1)} %get-tuple-element.10.k_ref, bf16[2,64,12,32,64]{4,3,2,1,0:T(8,128)(2,1)S(1)} %get-tuple-element.11.v_ref), custom_call_target="tpu_custom_call" | custom-call | tf_op jit(solution)/shard_map/pallas_call | solution.py:552

commit v3 on v2

--- a/solution.py
+++ b/solution.py
@@ -39,13 +39,13 @@
 YZX, ZX, XZ = (Y,) + ALONG_Z + (X,), ALONG_Z + (X,), (X,) + ALONG_Z
 SHARES = {
     'vec': [((1, ZXY),)],
-    'qkv': [((6, ZXY),), ((6, ZXY),)],
+    'qkv': [((5, ZXY), (1, YXZ)), ((6, ZXY),)],
     'out': [((6, ZXY),), ((6, ZXY),)],
     'win': [((3, YZX),)] * 2,
     'down': [((2, ZX), (1, XZ))] * 2,
 }
 GROUPS = tuple((f, l, i) for f, layers, n in (('vec', 1, 1), ('qkv', 2, 3), ('win', 2, 4), ('down', 2, 2), ('out', 2, 1)) for l in range(layers) for i in range(n))
-SEQUENCE = tuple(GROUPS[ord(k) - ord('a')] for k in 'tcbjakdligfhsequopmnr')
+SEQUENCE = tuple(GROUPS[ord(k) - ord('a')] for k in 'acfktgjibodephulqsnrm')
 
 
 def group_parts(family, l, i):
@@ -273,13 +273,15 @@
     def my_cols(zb, yy):
         return pl.ds(pl.multiple_of(768 * zb + 384 * yy, 128), 384)
 
-    own = [(qkv_ref.at[0], qkv_g.at[0, z, y, x, c])]
-    own += [(win_ref.at[0, :, my_cols(zb, y)], win_g.at[0, z, y, x, c, :, pl.ds(384 * zb, 384)]) for zb in range(4)]
-    own += [(down_ref.at[0], down_g.at[0, z, x, c]), (out_ref.at[0], out_g.at[0, z, y, x, c]), (qkv_ref.at[1], qkv_g.at[1, z, y, x, c])]
-    own += [(win_ref.at[1, :, my_cols(zb, y)], win_g.at[1, z, y, x, c, :, pl.ds(384 * zb, 384)]) for zb in range(4)]
-    own += [(down_ref.at[1], down_g.at[1, z, x, c]), (out_ref.at[1], out_g.at[1, z, y, x, c])]
-    own = [pltpu.make_async_copy(src, dst, own_sem.at[i]) for i, (src, dst) in enumerate(own)]
-    for cp in own:
+    own = {'vec0': []}
+    for l in range(2):
+        own[f'qkv{l}'] = [(qkv_ref.at[l], qkv_g.at[l, z, y, x, c])]
+        own[f'win{l}'] = [(win_ref.at[l, :, my_cols(zb, y)], win_g.at[l, z, y, x, c, :, pl.ds(384 * zb, 384)]) for zb in range(4)]
+        own[f'down{l}'] = [(down_ref.at[l], down_g.at[l, z, x, c])]
+        own[f'out{l}'] = [(out_ref.at[l], out_g.at[l, z, y, x, c])]
+    count = itertools.count()
+    own = {k: [pltpu.make_async_copy(src, dst, own_sem.at[next(count)]) for src, dst in v] for k, v in own.items()}
+    for cp in itertools.chain(*own.values()):
         cp.start()
 
     barrier = pltpu.get_barrier_semaphore()
@@ -298,8 +300,6 @@
         at_row += count
 
     pl.semaphore_wait(barrier, 3 + (z + 3) // 4 + (6 - z) // 4)
-    for cp in own:
-        cp.wait()
     refs = {'vec': vec_g, 'qkv': qkv_g, 'win': win_g, 'down': down_g, 'out': out_g}
     parts = []
     for i, (family, l, col, width, order) in enumerate(specs):
@@ -476,6 +476,9 @@
             tasks.pop(step)()
             continue
         p, phase = parts[step[0]], step[1]
+        if phase < 0:
+            for cp in own.pop(specs[step[0]][0] + str(specs[step[0]][1]), ()):
+                cp.wait()
         if phase >= 0:
             p.finish(phase)
         if phase + 1 < p.phases:

time: 111 us -> 113 us (1.018)
  Pallas kernels: 110 us -> 112 us
    pallas_call x1, Pallas kernels: 102 us -> 103 us  [fused(): pl.pallas_call(functools.partial(kernel, specs, steps), out_shape=tuple((...]
where the time goes in v3:
time: 113 us; the launch traced here: 112 us
  Pallas kernels  112 us (99%)
    pallas_call x1, Pallas kernels, fused(): pl.pallas_call(functools.partial(kernel, specs, steps), out_shape=tuple((...  103 us
    pallas_call x1, Pallas kernels, fused(): pl.pallas_call(write_kernel, out_shape=tuple((jax.ShapeDtypeStruct(a.shap...  8.55 us

profile of v3, /device:TPU:0, one launch (start us, length us, event | category | flops | bytes accessed | tf_op | source)
XLA Modules:
  0.0 112.5 jit_solution(6704502333339145120)
XLA Ops:
  0.6 103.1 %shard_map.193 = (bf16[64,768]{1,0:T(8,128)(2,1)S(1)}, bf16[2,64,12,32,64]{4,3,2,1,0:T(8,128)(2,1)S(1)}, bf16[2,64,12,32,64]{4,3,2,1,0:T(8,128)(2,1)S(1)}) custom-call(s32[64]{0:T(128)} %pos_ref.1, bf16[64,768]{1,0:T(8,128)(2,1)} %x_ref.1, bf16[2,24]{1,0:T(2,128)(2,1)} %g1_ref.1, bf16[2,24]{1,0:T(2,128)(2,1)} %c1_ref.1, bf16[2,24]{1,0:T(2,128)(2,1)} %g2_ref.1, ...), custom_call_target="tpu_custom_call" | custom-call | tf_op jit(solution)/shard_map/pallas_call | solution.py:522
  103.7 8.6 %shard_map.194 = (bf16[64,768]{1,0:T(8,128)(2,1)}, bf16[2,64,12,32,64]{4,3,2,1,0:T(8,128)(2,1)}, bf16[2,64,12,32,64]{4,3,2,1,0:T(8,128)(2,1)}) custom-call(bf16[64,768]{1,0:T(8,128)(2,1)S(1)} %get-tuple-element.9.y_ref, bf16[2,64,12,32,64]{4,3,2,1,0:T(8,128)(2,1)S(1)} %get-tuple-element.10.k_ref, bf16[2,64,12,32,64]{4,3,2,1,0:T(8,128)(2,1)S(1)} %get-tuple-element.11.v_ref), custom_call_target="tpu_custom_call" | custom-call | tf_op jit(solution)/shard_map/pallas_call | solution.py:555
